TPU v7x, 32 devices: a whole 2x2x4 slice. The times are simulated.
32 devices in a mesh: runs: 2 (over x), brick: 16 (over z, y, core).
Axes of the slice: x: 2, y: 2, z: 4, core: 2. Of those that a mesh axis runs over, the one named last changes fastest.
Arguments:
- grid: float32 [3, 8388608], P(None, ('runs', 'brick')), parts along dimension 1, may hold values from 0.2 to 4
- distribution: float32 [64, 16384], P(None, ('runs', 'brick')), parts along dimension 1, may hold values from 0.02 to 1
- owner_ids: int32 [16384, 1], P(('runs', 'brick')), parts along dimension 0, may hold values from 0 to 15; in each aligned block of 512 rows (0 to 511, 512 to 1023, ...) at most 64 rows name the same one
- coords: int32 [3, 16384], P(None, ('runs', 'brick')), parts along dimension 1, may hold values from 0 to 62
- fracs: float32 [3, 16384], P(None, ('runs', 'brick')), parts along dimension 1, may hold values from 0 to 1
- counts: int32 [16384], P(('runs', 'brick')), parts along dimension 0, may hold values from 1 to 4
- kernel: float32 [64, 64], replicated, may hold values from 0.002 to 0.2
- redist: float32 [64, 64], replicated, may hold values from 0.001 to 0.05
- shatter: float32 [64, 64], replicated, may hold values from 0.001 to 0.05
Outputs:
- updated: float32 [64, 16384], P(None, ('runs', 'brick')), parts along dimension 1
There are 2 independent parts, one for each index of `runs`. A program takes and returns all parts, laid end to end along the dimension named above; an argument that names none is the same for every part. Nothing has to cross between parts.
Inputs may be any that keep to these rules, and one draw needn't show every extreme that they name: `owner_ids`: in the rows of one device at most 64 tracers name one brick, a bound that some block reaches of them.
All inputs are finite; a program needn't handle non-finite values.
Results may differ from a plain program's by a relative error of at most 0.0001.
Values sent between devices are 32-bit elements; how exact they have to be, the bound alone decides.
No kernel may reach another device: no remote copies, remote signals or barrier semaphores. Data moves between devices by JAX's collectives and lax.ppermute only.
A program may use at most 256 MiB of HBM per device.

v0:
```python
import functools

import jax
import jax.numpy as jnp
from jax import lax
from jax.experimental import pallas as pl
from jax.experimental.pallas import tpu as pltpu
from jax.sharding import PartitionSpec as P

BS = 64
LANES = 128
ROWS_PER_TILE = LANES // BS
PLANE = BS * BS // LANES
NT = (((1,), (1,)), ((), ()))


def split3(x):
    hi = x.astype(jnp.bfloat16)
    rest = x - hi.astype(jnp.float32)
    mid = rest.astype(jnp.bfloat16)
    low = (rest - mid.astype(jnp.float32)).astype(jnp.bfloat16)
    return hi.astype(jnp.float32), mid.astype(jnp.float32), low.astype(jnp.float32)


def pack_kernel(
    bricks,
    capacity,
    owner_hbm,
    coords_hbm,
    fracs_hbm,
    request_ref,
    rank_ref,
    owner_ref,
    coords_ref,
    fracs_ref,
    sem,
):
    copies = [
        pltpu.make_async_copy(source, target, sem.at[c])
        for c, (source, target) in enumerate(
            ((owner_hbm, owner_ref), (coords_hbm, coords_ref), (fracs_hbm, fracs_ref))
        )
    ]
    for copy in copies:
        copy.start()
    for copy in copies:
        copy.wait()
    tracers = owner_ref.shape[1]
    groups = tracers // LANES
    owner = owner_ref[...]
    brick = lax.broadcasted_iota(jnp.int32, (bricks, LANES), 0)
    row = lax.broadcasted_iota(jnp.int32, (LANES, 2 * LANES), 0)
    column = lax.broadcasted_iota(jnp.int32, (LANES, 2 * LANES), 1)
    before = jnp.where((row < column) | (column >= LANES), 1.0, 0.0).astype(jnp.bfloat16)
    member = [
        jnp.where(owner[:, g * LANES : (g + 1) * LANES] == brick, 1.0, 0.0) for g in range(groups)
    ]
    counted = jnp.dot(
        jnp.concatenate(member, axis=0).astype(jnp.bfloat16),
        before,
        preferred_element_type=jnp.float32,
    )
    base = jnp.zeros((bricks, LANES), jnp.float32)
    ranks = []
    for g in range(groups):
        block = counted[g * bricks : (g + 1) * bricks]
        ranks.append(jnp.sum(member[g] * (block[:, :LANES] + base), axis=0, keepdims=True))
        base = base + block[:, LANES:]
    rank = jnp.concatenate(ranks, axis=1)
    rank_ref[...] = rank.astype(jnp.int32)
    place = lax.broadcasted_iota(jnp.int32, (LANES, tracers), 0) % capacity
    onehot = jnp.where(rank == place.astype(jnp.float32), 1.0, 0.0).astype(jnp.bfloat16)
    coords = coords_ref[...].astype(jnp.float32)
    hi, mid, low = split3(fracs_ref[...])
    one = jnp.zeros((1, tracers), jnp.float32)
    none = jnp.zeros((4, tracers), jnp.float32)
    parts = (
        jnp.concatenate([coords, one, hi, one], axis=0),
        jnp.concatenate([none, mid, one], axis=0),
        jnp.concatenate([none, low, one], axis=0),
    )
    total = None
    for part in parts:
        masked = jnp.concatenate(
            [jnp.where(owner == b, part, 0.0) for b in range(bricks)], axis=0
        ).astype(jnp.bfloat16)
        term = lax.dot_general(masked, onehot, NT, preferred_element_type=jnp.float32)
        total = term if total is None else total + term
    named = lax.broadcasted_iota(jnp.int32, (bricks, 8, LANES), 1) == 3
    request_ref[...] = jnp.where(named, base[:, None, :], total.reshape(bricks, 8, LANES))


def sample_kernel(
    bricks, capacity, request_ref, grid_ref, reply_ref, staged, where_ref, frac_ref, lines, sem
):
    blocks = 4 * capacity // LANES
    fractions = pltpu.make_async_copy(request_ref.at[:, 4, :], frac_ref, sem.at[0])
    fractions.start()
    asked = request_ref[...].astype(jnp.int32)
    second = jnp.concatenate([asked[:, 1:], asked[:, :1]], axis=1)
    shift = ROWS_PER_TILE.bit_length() - 1
    tile = asked * PLANE + (jnp.maximum(second - 1, 0) >> shift)
    turn = jnp.where(asked == 0, 0, jnp.where((asked & 1) == 1, BS, LANES))
    row = lax.broadcasted_iota(jnp.int32, asked.shape, 1)
    staged[...] = jnp.where(row == 0, tile, jnp.where(row == 1, turn, asked))
    copies = [
        pltpu.make_async_copy(staged.at[:, r, :], where_ref.at[c], sem.at[1 + c])
        for c, r in enumerate((0, 1, 3))
    ]
    for copy in copies:
        copy.start()
    lane = lax.broadcasted_iota(jnp.int32, (3, LANES), 1)
    fractions.wait()
    for copy in copies:
        copy.wait()
    chunk = 16

    def gather(p, carry):
        count = where_ref[2, p, 0]
        for c in range(0, capacity, chunk):

            @pl.when(count > c)
            def _():
                for r in range(c, c + chunk):
                    start = where_ref[0, p, r]
                    cut = lane < where_ref[1, p, r]
                    near = jnp.where(cut, grid_ref[start + 1], grid_ref[start])
                    far = jnp.where(cut, grid_ref[start + 1 + PLANE], grid_ref[start + PLANE])
                    line = near + frac_ref[p, r] * (far - near)
                    lines[pl.ds(p * (4 * capacity) + r, 3, stride=capacity), :] = line

        return carry

    lax.fori_loop(0, bricks, gather, 0)
    cell = lax.broadcasted_iota(jnp.int32, (BS, LANES), 0)

    def weigh(p):
        asked = request_ref[p]
        second = asked[1:2].astype(jnp.int32)
        third = asked[2:3].astype(jnp.int32)
        f1 = asked[5:6]
        f2 = asked[6:7]
        along = jnp.where(cell == third, 1.0 - f2, jnp.where(cell == third + 1, f2, 0.0))
        even = (second & 1) == 0
        top = jnp.where(even, 1.0 - f1, f1)
        bottom = jnp.where(even, f1, 1.0 - f1)
        rows = []
        for q in range(blocks):
            start = p * (4 * capacity) + q * LANES
            turned = lines[pl.ds(start, LANES), :].T
            crossed = turned[:BS] * top + turned[BS:] * bottom
            rows.append(jnp.sum(crossed * along, axis=0, keepdims=True))
        reply_ref[p] = jnp.concatenate(rows, axis=0)

    for p in range(bricks):
        weigh(p)


def advance_kernel(
    bricks,
    capacity,
    reply_ref,
    owner_ref,
    rank_ref,
    counts_ref,
    dist_ref,
    kernel_ref,
    redist_ref,
    shatter_ref,
    out_ref,
):
    tracers = owner_ref.shape[1]
    groups = tracers // LANES
    brick = lax.broadcasted_iota(jnp.int32, (bricks, LANES), 0)
    rows = [reply_ref[:, q, :] for q in range(reply_ref.shape[1])]
    fields = [[], [], []]
    for g in range(groups):
        lanes = slice(g * LANES, (g + 1) * LANES)
        mine = owner_ref[:, lanes] == brick
        rank = jnp.broadcast_to(rank_ref[:, lanes], (bricks, LANES))
        for f in range(3):
            q, offset = divmod(f * capacity, LANES)
            found = jnp.take_along_axis(rows[q], rank + offset, axis=1)
            fields[f].append(jnp.sum(jnp.where(mine, found, 0.0), axis=0, keepdims=True))
    density, temperature, metals = [jnp.concatenate(f, axis=1) for f in fields]
    coag = density * jnp.sqrt(temperature)
    shat = metals * temperature
    counts = counts_ref[...]
    h = 1.0 / jnp.maximum(counts, 1).astype(jnp.float32)

    def halves(x):
        hi = x.astype(jnp.bfloat16)
        return hi, (x - hi.astype(jnp.float32)).astype(jnp.bfloat16)

    def wide(x):
        hi, low = halves(x)
        return jnp.concatenate([hi, hi, low], axis=1)

    def tall(x):
        hi, low = halves(x)
        return jnp.concatenate([hi, low, hi], axis=0)

    def product(a, x):
        return jnp.dot(a, tall(x), preferred_element_type=jnp.float32)

    bins = dist_ref.shape[0]
    both = wide(jnp.concatenate([kernel_ref[...], shatter_ref[...]], axis=0))
    redist = wide(redist_ref[...])
    hcoag = h * coag
    hshat = h * shat
    n = dist_ref[...]
    for section in range(4):
        pair = product(both, n)
        kn = pair[:bins]
        broken = pair[bins:]
        moved = product(redist, n * kn)
        fresh = (n + (hcoag * moved + hshat * broken)) / (1.0 + (hcoag * kn + hshat))
        n = fresh if section == 0 else jnp.where(counts >= section + 1, fresh, n)
    out_ref[...] = n


def shards(grid, distribution, owner_ids, coords, fracs, counts, kernel, redist, shatter):
    bricks = lax.axis_size("brick")
    tracers = distribution.shape[1]
    capacity = 2 * tracers // bricks
    blocks = 4 * capacity // LANES
    owner = owner_ids.reshape(1, tracers)
    vmem = pl.BlockSpec(memory_space=pltpu.VMEM)
    request, rank = pl.pallas_call(
        functools.partial(pack_kernel, bricks, capacity),
        out_shape=(
            jax.ShapeDtypeStruct((bricks, 8, LANES), jnp.float32),
            jax.ShapeDtypeStruct((1, tracers), jnp.int32),
        ),
        in_specs=[pl.BlockSpec(memory_space=pltpu.HBM)] * 3,
        out_specs=(vmem, vmem),
        scratch_shapes=[
            pltpu.VMEM(owner.shape, owner.dtype),
            pltpu.VMEM(coords.shape, coords.dtype),
            pltpu.VMEM(fracs.shape, fracs.dtype),
            pltpu.SemaphoreType.DMA((3,)),
        ],
        cost_estimate=pl.CostEstimate(flops=20 << 30, bytes_accessed=1 << 20, transcendentals=0),
        compiler_params=pltpu.CompilerParams(vmem_limit_bytes=8 << 20),
        name="pack",
    )(*[pltpu.with_memory_space_constraint(x, pltpu.HBM) for x in (owner, coords, fracs)])
    asked = lax.all_to_all(request, "brick", split_axis=0, concat_axis=0, tiled=True)
    cells = grid.shape[1]
    tiles = grid.reshape(3, cells // LANES, LANES).transpose(1, 0, 2)
    reply = pl.pallas_call(
        functools.partial(sample_kernel, bricks, capacity),
        out_shape=jax.ShapeDtypeStruct((bricks, blocks, LANES), jnp.float32),
        in_specs=[vmem] * 2,
        out_specs=vmem,
        scratch_shapes=[
            pltpu.VMEM((bricks, 8, LANES), jnp.int32),
            pltpu.SMEM((3, bricks, LANES), jnp.int32),
            pltpu.SMEM((bricks, LANES), jnp.float32),
            pltpu.VMEM((bricks * 4 * capacity, LANES), jnp.float32),
            pltpu.SemaphoreType.DMA((4,)),
        ],
        compiler_params=pltpu.CompilerParams(vmem_limit_bytes=16 << 20),
        name="sample",
    )(asked, tiles)
    back = lax.all_to_all(reply, "brick", split_axis=0, concat_axis=0, tiled=True)
    return pl.pallas_call(
        functools.partial(advance_kernel, bricks, capacity),
        out_shape=jax.ShapeDtypeStruct(distribution.shape, jnp.float32),
        in_specs=[vmem] * 8,
        out_specs=vmem,
        compiler_params=pltpu.CompilerParams(vmem_limit_bytes=8 << 20),
        name="advance",
    )(back, owner, rank, counts.reshape(1, tracers), distribution, kernel, redist, shatter)


def solution(mesh):
    in_specs = (
        P(None, ("runs", "brick")),
        P(None, ("runs", "brick")),
        P(("runs", "brick"), None),
        P(None, ("runs", "brick")),
        P(None, ("runs", "brick")),
        P(("runs", "brick")),
        P(),
        P(),
        P(),
    )
    out_specs = P(None, ("runs", "brick"))
    return jax.shard_map(shards, mesh=mesh, in_specs=in_specs, out_specs=out_specs, check_vma=False)
```

profile of v0, /device:TPU:0, one launch (start us, length us, event | category | flops | bytes accessed | tf_op | source)
XLA Modules:
  0.0 30.5 jit_solution(4420944936072822719)
XLA Ops:
  0.0 0.0 copy-start
  0.0 1.3 %pack.1 = (f32[16,8,128]{2,1,0:T(8,128)S(1)}, s32[1,512]{1,0:T(1,128)S(1)}) custom-call(s32[1,512]{1,0:T(1,128)} %bitcast.6, s32[3,512]{1,0:T(4,128)} %coords_hbm.1, f32[3,512]{1,0:T(4,128)} %fracs_hbm.1), custom_call_target="tpu_custom_call" | custom-call | flops 21474836480 | bytes 1048576 | tf_op jit(solution)/shard_map/pack/pallas_call | solution.py:229
  1.3 0.0 copy-start.1
  1.4 0.0 copy-start.2
  1.4 0.0 copy-start.3
  1.4 0.0 copy-start.4
  1.4 0.0 copy-start.5
  1.4 0.0 copy-start.6
  1.4 14.2 %all_to_all.10.request_ref = f32[16,8,128]{2,1,0:T(8,128)S(1)} all-to-all(f32[16,8,128]{2,1,0:T(8,128)S(1)} %get-tuple-element.7), channel_id=1, replica_groups=mesh['runs'=2,'brick'=16] {'brick'}, dimensions={0} | all-to-all | bytes 131072 | tf_op jit(solution)/shard_map/all_to_all | solution.py:247
  15.7 0.0 copy-done
  15.7 3.4 %sample.1 = f32[16,2,128]{2,1,0:T(2,128)S(1)} custom-call(f32[16,8,128]{2,1,0:T(8,128)S(1)} %all_to_all.10.request_ref, f32[2048,3,128]{2,1,0:T(4,128)S(1)} %bitcast.5), custom_call_target="tpu_custom_call" | custom-call | tf_op jit(solution)/shard_map/sample/pallas_call | solution.py:250
  19.1 9.3 %all_to_all.11.reply_ref = f32[16,2,128]{2,1,0:T(2,128)S(1)} all-to-all(f32[16,2,128]{2,1,0:T(2,128)S(1)} %sample.1), channel_id=1, replica_groups=mesh['runs'=2,'brick'=16] {'brick'}, dimensions={0} | all-to-all | bytes 32768 | tf_op jit(solution)/shard_map/all_to_all | solution.py:265
  28.4 0.0 copy-done.1
  28.4 0.0 copy-done.2
  28.4 0.0 copy-done.3
  28.4 0.0 copy-done.4
  28.4 0.0 copy-done.5
  28.4 0.0 copy-done.6
  28.4 2.1 %advance.1 = f32[64,512]{1,0:T(8,128)} custom-call(f32[16,2,128]{2,1,0:T(2,128)S(1)} %all_to_all.11.reply_ref, s32[1,512]{1,0:T(1,128)S(1)} %bitcast.7, s32[1,512]{1,0:T(1,128)S(1)} %get-tuple-element.8.rank_ref, s32[1,512]{1,0:T(1,128)S(1)} %bitcast.8, f32[64,512]{1,0:T(8,128)S(1)} %copy-done.1, f32[64,64]{1,0:T(8,128)S(1)} %copy-done.2, ...), custom_call_target="tpu_custom_call" | custom-call | tf_op jit(solution)/shard_map/advance/pallas_call | solution.py:266
Async XLA Ops:
  0.0 15.7 %copy-start = (f32[3,262144]{1,0:T(4,128)S(1)}, f32[3,262144]{1,0:T(4,128)}, u32[]{:S(2)}) copy-start(f32[3,262144]{1,0:T(4,128)} %param.9) | copy-start | bytes 9437188
  1.3 27.0 %copy-start.1 = (f32[64,512]{1,0:T(8,128)S(1)}, f32[64,512]{1,0:T(8,128)}, u32[]{:S(2)}) copy-start(f32[64,512]{1,0:T(8,128)} %dist_ref.1) | copy-start | bytes 393220
  1.4 27.0 %copy-start.2 = (f32[64,64]{1,0:T(8,128)S(1)}, f32[64,64]{1,0:T(8,128)}, u32[]{:S(2)}) copy-start(f32[64,64]{1,0:T(8,128)} %kernel_ref.1) | copy-start | bytes 49156
  1.4 27.0 %copy-start.3 = (f32[64,64]{1,0:T(8,128)S(1)}, f32[64,64]{1,0:T(8,128)}, u32[]{:S(2)}) copy-start(f32[64,64]{1,0:T(8,128)} %redist_ref.1) | copy-start | bytes 49156
  1.4 27.0 %copy-start.4 = (f32[64,64]{1,0:T(8,128)S(1)}, f32[64,64]{1,0:T(8,128)}, u32[]{:S(2)}) copy-start(f32[64,64]{1,0:T(8,128)} %shatter_ref.1) | copy-start | bytes 49156
  1.4 27.0 %copy-start.5 = (s32[512,1]{0,1:T(1,128)S(1)}, s32[512,1]{0,1:T(1,128)}, u32[]{:S(2)}) copy-start(s32[512,1]{0,1:T(1,128)} %param.11) | copy-start | bytes 6148
  1.4 27.0 %copy-start.6 = (s32[512]{0:T(512)S(1)}, s32[512]{0:T(512)}, u32[]{:S(2)}) copy-start(s32[512]{0:T(512)} %param.14) | copy-start | bytes 6148
where the time goes:
time: 30.9 us; the launch traced here: 30.5 us
  blocking collectives  23.5 us (76%)
  Pallas kernels  6.82 us (22%)
    all_to_all x1, blocking collectives, shards(): lax.all_to_all(request, 'brick', split_axis=0, concat_axis=0, tiled=True)  14.2 us
    all_to_all x1, blocking collectives, shards(): lax.all_to_all(reply, 'brick', split_axis=0, concat_axis=0, tiled=True)  9.27 us
    pallas_call x1, Pallas kernels, shards(): pl.pallas_call(functools.partial(sample_kernel, bricks, capacity), out_sh...  3.42 us
    pallas_call x1, Pallas kernels, shards(): pl.pallas_call(functools.partial(advance_kernel, bricks, capacity), out_s...  2.07 us
    pallas_call x1, Pallas kernels, shards(): pl.pallas_call(functools.partial(pack_kernel, bricks, capacity), out_shap...  1.34 us

commit v1 on v0

v1 whole, which is shorter than its diff:
```python
import functools

import jax
import jax.numpy as jnp
from jax import lax
from jax.experimental import pallas as pl
from jax.experimental.pallas import tpu as pltpu
from jax.sharding import PartitionSpec as P

BS = 64
LANES = 128
ROWS_PER_TILE = LANES // BS
PLANE = BS * BS // LANES
TURN = 1 << 24
NT = (((1,), (1,)), ((), ()))


def split3(x):
    hi = x.astype(jnp.bfloat16)
    rest = x - hi.astype(jnp.float32)
    mid = rest.astype(jnp.bfloat16)
    low = (rest - mid.astype(jnp.float32)).astype(jnp.bfloat16)
    return hi.astype(jnp.float32), mid.astype(jnp.float32), low.astype(jnp.float32)


def halves(x):
    hi = x.astype(jnp.bfloat16)
    return hi, (x - hi.astype(jnp.float32)).astype(jnp.bfloat16)


def wide(x):
    hi, low = halves(x)
    return jnp.concatenate([hi, hi, low], axis=1)


def product(a, x):
    hi, low = halves(x)
    tall = jnp.concatenate([hi, low, hi], axis=0)
    return jnp.dot(a, tall, preferred_element_type=jnp.float32)


def tables(kernel_ref, redist_ref, shatter_ref):
    both = jnp.concatenate([kernel_ref[...], shatter_ref[...]], axis=0)
    return wide(both), wide(redist_ref[...])


def collide(both, redist, n):
    pair = product(both, n)
    kn = pair[: n.shape[0]]
    return kn, pair[n.shape[0] :], product(redist, n * kn)


def pack_kernel(
    bricks,
    capacity,
    owner_hbm,
    coords_hbm,
    fracs_hbm,
    request_ref,
    rank_ref,
    owner_ref,
    coords_ref,
    fracs_ref,
    sem,
):
    copies = [
        pltpu.make_async_copy(source, target, sem.at[c])
        for c, (source, target) in enumerate(
            ((owner_hbm, owner_ref), (coords_hbm, coords_ref), (fracs_hbm, fracs_ref))
        )
    ]
    for copy in copies:
        copy.start()
    tracers = owner_ref.shape[1]
    groups = tracers // LANES
    brick = lax.broadcasted_iota(jnp.int32, (bricks, LANES), 0)
    row = lax.broadcasted_iota(jnp.int32, (LANES, 2 * LANES), 0)
    column = lax.broadcasted_iota(jnp.int32, (LANES, 2 * LANES), 1)
    before = jnp.where((row < column) | (column >= LANES), 1.0, 0.0).astype(jnp.bfloat16)
    place = lax.broadcasted_iota(jnp.int32, (LANES, tracers), 0) % capacity
    place = place.astype(jnp.float32)
    copies[0].wait()
    owner = owner_ref[...]
    member = [
        jnp.where(owner[:, g * LANES : (g + 1) * LANES] == brick, 1.0, 0.0) for g in range(groups)
    ]
    counted = jnp.dot(
        jnp.concatenate(member, axis=0).astype(jnp.bfloat16),
        before,
        preferred_element_type=jnp.float32,
    )
    base = jnp.zeros((bricks, LANES), jnp.float32)
    ranks = []
    for g in range(groups):
        block = counted[g * bricks : (g + 1) * bricks]
        ranks.append(jnp.sum(member[g] * (block[:, :LANES] + base), axis=0, keepdims=True))
        base = base + block[:, LANES:]
    rank = jnp.concatenate(ranks, axis=1)
    rank_ref[...] = rank.astype(jnp.int32)
    onehot = jnp.where(rank == place, 1.0, 0.0).astype(jnp.bfloat16)
    copies[1].wait()
    copies[2].wait()
    coords = coords_ref[...].astype(jnp.float32)
    hi, mid, low = split3(fracs_ref[...])
    one = jnp.zeros((1, tracers), jnp.float32)
    none = jnp.zeros((4, tracers), jnp.float32)
    parts = (
        jnp.concatenate([coords, one, hi, one], axis=0),
        jnp.concatenate([none, mid, one], axis=0),
        jnp.concatenate([none, low, one], axis=0),
    )
    total = None
    for part in parts:
        masked = jnp.concatenate(
            [jnp.where(owner == b, part, 0.0) for b in range(bricks)], axis=0
        ).astype(jnp.bfloat16)
        term = lax.dot_general(masked, onehot, NT, preferred_element_type=jnp.float32)
        total = term if total is None else total + term
    request_ref[...] = total.reshape(bricks, 8, LANES)


def sample_kernel(
    bricks,
    capacity,
    request_ref,
    grid_ref,
    dist_ref,
    kernel_ref,
    redist_ref,
    shatter_ref,
    reply_ref,
    first_ref,
    staged,
    code_ref,
    frac_ref,
    lines,
    sem,
):
    shift = ROWS_PER_TILE.bit_length() - 1
    step = 2
    spans = (pl.ds(0, step), pl.ds(step, bricks - step))
    early, late = copies = ([], [])

    def fetch(c, source, target):
        for k, span in enumerate(spans):
            copy = pltpu.make_async_copy(source(span), target.at[span], sem.at[k, c])
            copy.start()
            copies[k].append(copy)

    fetch(0, lambda span: request_ref.at[span, 4, :], frac_ref)
    asked = request_ref[...].astype(jnp.int32)
    second = jnp.concatenate([asked[:, 1:], asked[:, :1]], axis=1)
    tile = asked * PLANE + (jnp.maximum(second - 1, 0) >> shift)
    turn = jnp.where(second == 0, 0, jnp.where((second & 1) == 1, 1, 2))
    staged[...] = turn * TURN + tile
    fetch(1, lambda span: staged.at[span, 0, :], code_ref)
    side = jnp.where(lax.broadcasted_iota(jnp.int32, (3, LANES), 1) < BS, TURN, 2 * TURN)
    cell = lax.broadcasted_iota(jnp.int32, (BS, LANES), 0)
    pitch = capacity + 8
    height = 3 * pitch

    shared = 3 * capacity > LANES
    half = lax.broadcasted_iota(jnp.int32, (1, LANES), 1) < capacity

    def weights(p):
        asked = request_ref[p]
        second = asked[1:2].astype(jnp.int32)
        third = asked[2:3].astype(jnp.int32)
        f1 = asked[5:6]
        f2 = asked[6:7]
        along = jnp.where(cell == third, 1.0 - f2, jnp.where(cell == third + 1, f2, 0.0))
        even = (second & 1) == 0
        top = jnp.where(even, 1.0 - f1, f1)
        bottom = jnp.where(even, f1, 1.0 - f1)
        return top, bottom, along

    def weigh(pieces, factors):
        top, bottom, along = factors
        block = [lines[pl.ds(p * height + f * pitch, capacity), :] for p, f in pieces]
        used = len(block) * capacity
        turned = jnp.concatenate(block, axis=0).T
        crossed = turned[:BS] * top[:, :used] + turned[BS:] * bottom[:, :used]
        return jnp.sum(crossed * along[:, :used], axis=0, keepdims=True)

    def settle(p):
        factors = [weights(p + u) for u in range(step)]
        for u in range(step):
            fields = range(2 if shared else 3)
            total = weigh([(p + u, f) for f in fields], factors[u])
            reply_ref[p + u, 0:1, : total.shape[1]] = total
        if shared:
            mixed = [jnp.where(half, a, b) for a, b in zip(*factors)]
            total = weigh([(p + u, 2) for u in range(step)], mixed)
            for u in range(step):
                reply_ref[p + u, 1:2, :] = total

    bins = dist_ref.shape[0]
    both, redist = tables(kernel_ref, redist_ref, shatter_ref)
    for k, value in enumerate(collide(both, redist, dist_ref[...])):
        first_ref[k * bins : (k + 1) * bins] = value
    for copy in early:
        copy.wait()

    def gather(p):
        for r in range(capacity):
            code = code_ref[p, r]
            start = code & (TURN - 1)
            cut = code >= side
            near = jnp.where(cut, grid_ref[start + 1], grid_ref[start])
            far = jnp.where(cut, grid_ref[start + 1 + PLANE], grid_ref[start + PLANE])
            line = near + frac_ref[p, r] * (far - near)
            lines[pl.ds(p * height + r, 3, stride=pitch), :] = line

    def peers(q, carry):
        @pl.when(q == 1)
        def _():
            for copy in late:
                copy.wait()

        settle(jnp.maximum(step * (q - 1), 0))
        for u in range(step):
            gather(step * q + u)
        return carry

    lax.fori_loop(0, bricks // step, peers, 0)
    settle(bricks - step)


def advance_kernel(
    bricks,
    capacity,
    reply_ref,
    first_ref,
    owner_ref,
    rank_ref,
    counts_ref,
    dist_ref,
    kernel_ref,
    redist_ref,
    shatter_ref,
    out_ref,
):
    tracers = owner_ref.shape[1]
    groups = tracers // LANES
    brick = lax.broadcasted_iota(jnp.int32, (bricks, LANES), 0)
    rows = [reply_ref[:, q, :] for q in range(reply_ref.shape[1])]
    fields = [[], [], []]
    for g in range(groups):
        lanes = slice(g * LANES, (g + 1) * LANES)
        mine = owner_ref[:, lanes] == brick
        rank = jnp.broadcast_to(rank_ref[:, lanes], (bricks, LANES))
        for f in range(3):
            q, offset = divmod(f * capacity, LANES)
            if q:
                offset = capacity * (lax.axis_index("brick") % 2)
            found = jnp.take_along_axis(rows[q], rank + offset, axis=1)
            fields[f].append(jnp.sum(jnp.where(mine, found, 0.0), axis=0, keepdims=True))
    density, temperature, metals = [jnp.concatenate(f, axis=1) for f in fields]
    coag = density * jnp.sqrt(temperature)
    shat = metals * temperature
    counts = counts_ref[...]
    h = 1.0 / jnp.maximum(counts, 1).astype(jnp.float32)

    bins = dist_ref.shape[0]
    both, redist = tables(kernel_ref, redist_ref, shatter_ref)
    hcoag = h * coag
    hshat = h * shat
    n = dist_ref[...]
    for section in range(4):
        if section == 0:
            kn, broken, moved = (first_ref[k * bins : (k + 1) * bins] for k in range(3))
        else:
            kn, broken, moved = collide(both, redist, n)
        fresh = (n + (hcoag * moved + hshat * broken)) / (1.0 + (hcoag * kn + hshat))
        n = fresh if section == 0 else jnp.where(counts >= section + 1, fresh, n)
    out_ref[...] = n


def shards(grid, distribution, owner_ids, coords, fracs, counts, kernel, redist, shatter):
    bricks = lax.axis_size("brick")
    tracers = distribution.shape[1]
    capacity = 2 * tracers // bricks
    blocks = 4 * capacity // LANES
    owner = owner_ids.reshape(1, tracers)
    vmem = pl.BlockSpec(memory_space=pltpu.VMEM)
    request, rank = pl.pallas_call(
        functools.partial(pack_kernel, bricks, capacity),
        out_shape=(
            jax.ShapeDtypeStruct((bricks, 8, LANES), jnp.float32),
            jax.ShapeDtypeStruct((1, tracers), jnp.int32),
        ),
        in_specs=[pl.BlockSpec(memory_space=pltpu.HBM)] * 3,
        out_specs=(vmem, vmem),
        scratch_shapes=[
            pltpu.VMEM(owner.shape, owner.dtype),
            pltpu.VMEM(coords.shape, coords.dtype),
            pltpu.VMEM(fracs.shape, fracs.dtype),
            pltpu.SemaphoreType.DMA((3,)),
        ],
        cost_estimate=pl.CostEstimate(flops=20 << 30, bytes_accessed=1 << 20, transcendentals=0),
        compiler_params=pltpu.CompilerParams(vmem_limit_bytes=8 << 20),
        name="pack",
    )(*[pltpu.with_memory_space_constraint(x, pltpu.HBM) for x in (owner, coords, fracs)])
    asked = lax.all_to_all(request, "brick", split_axis=0, concat_axis=0, tiled=True)
    cells = grid.shape[1]
    tiles = grid.reshape(3, cells // LANES, LANES).transpose(1, 0, 2)
    reply, first = pl.pallas_call(
        functools.partial(sample_kernel, bricks, capacity),
        out_shape=(
            jax.ShapeDtypeStruct((bricks, blocks, LANES), jnp.float32),
            jax.ShapeDtypeStruct((3 * distribution.shape[0], tracers), jnp.float32),
        ),
        in_specs=[vmem] * 6,
        out_specs=(vmem, vmem),
        scratch_shapes=[
            pltpu.VMEM((bricks, 8, LANES), jnp.int32),
            pltpu.SMEM((bricks, LANES), jnp.int32),
            pltpu.SMEM((bricks, LANES), jnp.float32),
            pltpu.VMEM((bricks * 3 * (capacity + 8), LANES), jnp.float32),
            pltpu.SemaphoreType.DMA((2, 2)),
        ],
        compiler_params=pltpu.CompilerParams(vmem_limit_bytes=16 << 20),
        name="sample",
    )(asked, tiles, distribution, kernel, redist, shatter)
    back = lax.all_to_all(reply, "brick", split_axis=0, concat_axis=0, tiled=True)
    return pl.pallas_call(
        functools.partial(advance_kernel, bricks, capacity),
        out_shape=jax.ShapeDtypeStruct(distribution.shape, jnp.float32),
        in_specs=[vmem] * 9,
        out_specs=vmem,
        compiler_params=pltpu.CompilerParams(vmem_limit_bytes=8 << 20),
        name="advance",
    )(back, first, owner, rank, counts.reshape(1, tracers), distribution, kernel, redist, shatter)


def solution(mesh):
    in_specs = (
        P(None, ("runs", "brick")),
        P(None, ("runs", "brick")),
        P(("runs", "brick"), None),
        P(None, ("runs", "brick")),
        P(None, ("runs", "brick")),
        P(("runs", "brick")),
        P(),
        P(),
        P(),
    )
    out_specs = P(None, ("runs", "brick"))
    return jax.shard_map(shards, mesh=mesh, in_specs=in_specs, out_specs=out_specs, check_vma=False)
```

time: 30.9 us -> 29.8 us (0.964)
  Pallas kernels: 6.82 us -> 6.16 us
    pallas_call x1, Pallas kernels: 3.42 us -> 3 us  [shards(): pl.pallas_call(functools.partial(sample_kernel, bricks, capacity), out_sh...]
where the time goes in v1:
time: 29.8 us; the launch traced here: 29.6 us
  blocking collectives  23.3 us (78%)
  Pallas kernels  6.16 us (21%)
    all_to_all x1, blocking collectives, shards(): lax.all_to_all(request, 'brick', split_axis=0, concat_axis=0, tiled=True)  14.3 us
    all_to_all x1, blocking collectives, shards(): lax.all_to_all(reply, 'brick', split_axis=0, concat_axis=0, tiled=True)  9.07 us
    pallas_call x1, Pallas kernels, shards(): pl.pallas_call(functools.partial(sample_kernel, bricks, capacity), out_sh...  3 us
    pallas_call x1, Pallas kernels, shards(): pl.pallas_call(functools.partial(advance_kernel, bricks, capacity), out_s...  1.85 us
    pallas_call x1, Pallas kernels, shards(): pl.pallas_call(functools.partial(pack_kernel, bricks, capacity), out_shap...  1.31 us

profile of v1, /device:TPU:0, one launch (start us, length us, event | category | flops | bytes accessed | tf_op | source)
XLA Modules:
  0.0 29.6 jit_solution(16943838187730737752)
XLA Ops:
  0.0 0.0 copy-start
  0.0 0.0 copy-start.1
  0.0 0.0 copy-start.2
  0.0 0.0 copy-start.3
  0.0 0.0 copy-start.4
  0.0 1.3 %pack.1 = (f32[16,8,128]{2,1,0:T(8,128)S(1)}, s32[1,512]{1,0:T(1,128)S(1)}) custom-call(s32[1,512]{1,0:T(1,128)} %bitcast.6, s32[3,512]{1,0:T(4,128)} %coords_hbm.1, f32[3,512]{1,0:T(4,128)} %fracs_hbm.1), custom_call_target="tpu_custom_call" | custom-call | flops 21474836480 | bytes 1048576 | tf_op jit(solution)/shard_map/pack/pallas_call | solution.py:286
  1.3 0.0 copy-start.5
  1.3 0.0 copy-start.6
  1.4 14.3 %all_to_all.10.request_ref = f32[16,8,128]{2,1,0:T(8,128)S(1)} all-to-all(f32[16,8,128]{2,1,0:T(8,128)S(1)} %get-tuple-element.9), channel_id=1, replica_groups=mesh['runs'=2,'brick'=16] {'brick'}, dimensions={0} | all-to-all | bytes 131072 | tf_op jit(solution)/shard_map/all_to_all | solution.py:304
  15.6 0.0 copy-done
  15.6 0.0 copy-done.1
  15.6 0.0 copy-done.2
  15.6 0.0 copy-done.3
  15.6 0.0 copy-done.4
  15.7 3.0 %sample.1 = (f32[16,2,128]{2,1,0:T(2,128)S(1)}, f32[192,512]{1,0:T(8,128)S(1)}) custom-call(f32[16,8,128]{2,1,0:T(8,128)S(1)} %all_to_all.10.request_ref, f32[2048,3,128]{2,1,0:T(4,128)S(1)} %bitcast.5, f32[64,512]{1,0:T(8,128)S(1)} %copy-done.1, f32[64,64]{1,0:T(8,128)S(1)} %copy-done.2, f32[64,64]{1,0:T(8,128)S(1)} %copy-done.3, f32[64,64]{1,0:T(8,128)S(1)} %copy-done.4), custom_call_target="tpu_custom_call" | custom-call | tf_op jit(solution)/shard_map/sample/pallas_call | solution.py:307
  18.7 9.1 %all_to_all.11.reply_ref = f32[16,2,128]{2,1,0:T(2,128)S(1)} all-to-all(f32[16,2,128]{2,1,0:T(2,128)S(1)} %get-tuple-element.10), channel_id=1, replica_groups=mesh['runs'=2,'brick'=16] {'brick'}, dimensions={0} | all-to-all | bytes 32768 | tf_op jit(solution)/shard_map/all_to_all | solution.py:325
  27.7 0.0 copy-done.5
  27.7 0.0 copy-done.6
  27.7 1.9 %advance.1 = f32[64,512]{1,0:T(8,128)} custom-call(f32[16,2,128]{2,1,0:T(2,128)S(1)} %all_to_all.11.reply_ref, f32[192,512]{1,0:T(8,128)S(1)} %get-tuple-element.11.first_ref, s32[1,512]{1,0:T(1,128)S(1)} %bitcast.7, s32[1,512]{1,0:T(1,128)S(1)} %get-tuple-element.12.rank_ref, s32[1,512]{1,0:T(1,128)S(1)} %bitcast.8, f32[64,512]{1,0:T(8,128)S(1)} %copy-done.1, ...), custom_call_target="tpu_custom_call" | custom-call | tf_op jit(solution)/shard_map/advance/pallas_call | solution.py:326
Async XLA Ops:
  0.0 15.6 %copy-start = (f32[3,262144]{1,0:T(4,128)S(1)}, f32[3,262144]{1,0:T(4,128)}, u32[]{:S(2)}) copy-start(f32[3,262144]{1,0:T(4,128)} %param.9) | copy-start | bytes 9437188
  0.0 15.6 %copy-start.1 = (f32[64,512]{1,0:T(8,128)S(1)}, f32[64,512]{1,0:T(8,128)}, u32[]{:S(2)}) copy-start(f32[64,512]{1,0:T(8,128)} %dist_ref.3) | copy-start | bytes 393220
  0.0 15.6 %copy-start.2 = (f32[64,64]{1,0:T(8,128)S(1)}, f32[64,64]{1,0:T(8,128)}, u32[]{:S(2)}) copy-start(f32[64,64]{1,0:T(8,128)} %kernel_ref.3) | copy-start | bytes 49156
  0.0 15.6 %copy-start.3 = (f32[64,64]{1,0:T(8,128)S(1)}, f32[64,64]{1,0:T(8,128)}, u32[]{:S(2)}) copy-start(f32[64,64]{1,0:T(8,128)} %redist_ref.3) | copy-start | bytes 49156
  0.0 15.6 %copy-start.4 = (f32[64,64]{1,0:T(8,128)S(1)}, f32[64,64]{1,0:T(8,128)}, u32[]{:S(2)}) copy-start(f32[64,64]{1,0:T(8,128)} %shatter_ref.3) | copy-start | bytes 49156
  1.3 26.4 %copy-start.5 = (s32[512,1]{0,1:T(1,128)S(1)}, s32[512,1]{0,1:T(1,128)}, u32[]{:S(2)}) copy-start(s32[512,1]{0,1:T(1,128)} %param.11) | copy-start | bytes 6148
  1.3 26.4 %copy-start.6 = (s32[512]{0:T(512)S(1)}, s32[512]{0:T(512)}, u32[]{:S(2)}) copy-start(s32[512]{0:T(512)} %param.14) | copy-start | bytes 6148

commit v2 on v1

--- a/solution.py
+++ b/solution.py
@@ -9,6 +9,7 @@
 
 BS = 64
 LANES = 128
+HALF = LANES // 2
 ROWS_PER_TILE = LANES // BS
 PLANE = BS * BS // LANES
 TURN = 1 << 24
@@ -77,8 +78,11 @@
     row = lax.broadcasted_iota(jnp.int32, (LANES, 2 * LANES), 0)
     column = lax.broadcasted_iota(jnp.int32, (LANES, 2 * LANES), 1)
     before = jnp.where((row < column) | (column >= LANES), 1.0, 0.0).astype(jnp.bfloat16)
-    place = lax.broadcasted_iota(jnp.int32, (LANES, tracers), 0) % capacity
-    place = place.astype(jnp.float32)
+    lane = lax.broadcasted_iota(jnp.int32, (LANES, tracers), 0)
+    place = (lane % capacity).astype(jnp.float32)
+    left = lane < HALF
+    nobody = jnp.full((LANES, tracers), -1.0, jnp.float32)
+    places = (jnp.where(left, place, nobody), jnp.where(left, nobody, place))
     copies[0].wait()
     owner = owner_ref[...]
     member = [
@@ -97,26 +101,28 @@
         base = base + block[:, LANES:]
     rank = jnp.concatenate(ranks, axis=1)
     rank_ref[...] = rank.astype(jnp.int32)
-    onehot = jnp.where(rank == place, 1.0, 0.0).astype(jnp.bfloat16)
+    places = [jnp.where(rank == x, 1.0, 0.0).astype(jnp.bfloat16) for x in places]
     copies[1].wait()
     copies[2].wait()
     coords = coords_ref[...].astype(jnp.float32)
     hi, mid, low = split3(fracs_ref[...])
-    one = jnp.zeros((1, tracers), jnp.float32)
-    none = jnp.zeros((4, tracers), jnp.float32)
-    parts = (
-        jnp.concatenate([coords, one, hi, one], axis=0),
-        jnp.concatenate([none, mid, one], axis=0),
-        jnp.concatenate([none, low, one], axis=0),
-    )
+    none = jnp.zeros((3, tracers), jnp.float32)
+    rows = bricks * 4
+    mine = owner == lax.broadcasted_iota(jnp.int32, (rows, tracers), 0) // 4
     total = None
-    for part in parts:
-        masked = jnp.concatenate(
-            [jnp.where(owner == b, part, 0.0) for b in range(bricks)], axis=0
-        ).astype(jnp.bfloat16)
-        term = lax.dot_general(masked, onehot, NT, preferred_element_type=jnp.float32)
-        total = term if total is None else total + term
-    request_ref[...] = total.reshape(bricks, 8, LANES)
+    for x in (hi, mid, low):
+        first = coords if total is None else none
+        for onehot, lines in ((0, (first, x[:1])), (1, (x[1:], none[:2]))):
+            block = jnp.concatenate(lines, axis=0)
+            pair = jnp.concatenate([block, block], axis=0)
+            masked = jnp.concatenate([pair] * (bricks // 2), axis=0)
+            masked = jnp.where(mine, masked, 0.0).astype(jnp.bfloat16)
+            term = lax.dot_general(
+                masked, places[onehot], NT, preferred_element_type=jnp.float32
+            )
+            total = term if total is None else total + term
+    for b in range(bricks):
+        request_ref[b] = total[4 * b : 4 * b + 4]
 
 
 def sample_kernel(
@@ -133,6 +139,7 @@
     staged,
     code_ref,
     frac_ref,
+    both_ref,
     lines,
     sem,
 ):
@@ -147,7 +154,7 @@
             copy.start()
             copies[k].append(copy)
 
-    fetch(0, lambda span: request_ref.at[span, 4, :], frac_ref)
+    fetch(0, lambda span: request_ref.at[span, 3, :], frac_ref)
     asked = request_ref[...].astype(jnp.int32)
     second = jnp.concatenate([asked[:, 1:], asked[:, :1]], axis=1)
     tile = asked * PLANE + (jnp.maximum(second - 1, 0) >> shift)
@@ -155,7 +162,7 @@
     staged[...] = turn * TURN + tile
     fetch(1, lambda span: staged.at[span, 0, :], code_ref)
     side = jnp.where(lax.broadcasted_iota(jnp.int32, (3, LANES), 1) < BS, TURN, 2 * TURN)
-    cell = lax.broadcasted_iota(jnp.int32, (BS, LANES), 0)
+    cell = lax.broadcasted_iota(jnp.int32, (BS, LANES), 0).astype(jnp.float32)
     pitch = capacity + 8
     height = 3 * pitch
 
@@ -163,12 +170,14 @@
     half = lax.broadcasted_iota(jnp.int32, (1, LANES), 1) < capacity
 
     def weights(p):
-        asked = request_ref[p]
+        here = request_ref[p]
+        turned = jnp.concatenate([here[:, HALF:], here[:, :HALF]], axis=1)
+        asked = jnp.concatenate([jnp.where(former, here, turned), jnp.where(former, turned, here)], axis=0)
         second = asked[1:2].astype(jnp.int32)
-        third = asked[2:3].astype(jnp.int32)
-        f1 = asked[5:6]
-        f2 = asked[6:7]
-        along = jnp.where(cell == third, 1.0 - f2, jnp.where(cell == third + 1, f2, 0.0))
+        third = asked[2:3]
+        f1 = asked[4:5]
+        f2 = asked[5:6]
+        along = jnp.where(cell == third, 1.0 - f2, jnp.where(cell == third + 1.0, f2, 0.0))
         even = (second & 1) == 0
         top = jnp.where(even, 1.0 - f1, f1)
         bottom = jnp.where(even, f1, 1.0 - f1)
@@ -194,6 +203,7 @@
             for u in range(step):
                 reply_ref[p + u, 1:2, :] = total
 
+    former = lax.broadcasted_iota(jnp.int32, (4, LANES), 1) < HALF
     bins = dist_ref.shape[0]
     both, redist = tables(kernel_ref, redist_ref, shatter_ref)
     for k, value in enumerate(collide(both, redist, dist_ref[...])):
@@ -286,7 +296,7 @@
     request, rank = pl.pallas_call(
         functools.partial(pack_kernel, bricks, capacity),
         out_shape=(
-            jax.ShapeDtypeStruct((bricks, 8, LANES), jnp.float32),
+            jax.ShapeDtypeStruct((bricks, 4, LANES), jnp.float32),
             jax.ShapeDtypeStruct((1, tracers), jnp.int32),
         ),
         in_specs=[pl.BlockSpec(memory_space=pltpu.HBM)] * 3,
@@ -313,9 +323,10 @@
         in_specs=[vmem] * 6,
         out_specs=(vmem, vmem),
         scratch_shapes=[
-            pltpu.VMEM((bricks, 8, LANES), jnp.int32),
+            pltpu.VMEM((bricks, 4, LANES), jnp.int32),
             pltpu.SMEM((bricks, LANES), jnp.int32),
             pltpu.SMEM((bricks, LANES), jnp.float32),
+            pltpu.VMEM((bricks, 8, LANES), jnp.float32),
             pltpu.VMEM((bricks * 3 * (capacity + 8), LANES), jnp.float32),
             pltpu.SemaphoreType.DMA((2, 2)),
         ],

time: 29.8 us -> 29.6 us (level)
  blocking collectives: 23.3 us -> 22.9 us
    all_to_all x1, blocking collectives: 14.3 us -> 13.9 us  [shards(): lax.all_to_all(request, 'brick', split_axis=0, concat_axis=0, tiled=True)]
where the time goes in v2:
time: 29.6 us; the launch traced here: 29.4 us
  blocking collectives  22.9 us (77%)
  Pallas kernels  6.35 us (21%)
    all_to_all x1, blocking collectives, shards(): lax.all_to_all(request, 'brick', split_axis=0, concat_axis=0, tiled=True)  13.9 us
    all_to_all x1, blocking collectives, shards(): lax.all_to_all(reply, 'brick', split_axis=0, concat_axis=0, tiled=True)  9.07 us
    pallas_call x1, Pallas kernels, shards(): pl.pallas_call(functools.partial(sample_kernel, bricks, capacity), out_sh...  3.09 us
    pallas_call x1, Pallas kernels, shards(): pl.pallas_call(functools.partial(advance_kernel, bricks, capacity), out_s...  1.86 us
    pallas_call x1, Pallas kernels, shards(): pl.pallas_call(functools.partial(pack_kernel, bricks, capacity), out_shap...  1.41 us

profile of v2, /device:TPU:0, one launch (start us, length us, event | category | flops | bytes accessed | tf_op | source)
XLA Modules:
  0.0 29.4 jit_solution(14786846714305634597)
XLA Ops:
  0.0 0.0 copy-start
  0.0 0.0 copy-start.1
  0.0 0.0 copy-start.2
  0.0 0.0 copy-start.3
  0.0 0.0 copy-start.4
  0.0 1.4 %pack.1 = (f32[16,4,128]{2,1,0:T(4,128)S(1)}, s32[1,512]{1,0:T(1,128)S(1)}) custom-call(s32[1,512]{1,0:T(1,128)} %bitcast.6, s32[3,512]{1,0:T(4,128)} %coords_hbm.1, f32[3,512]{1,0:T(4,128)} %fracs_hbm.1), custom_call_target="tpu_custom_call" | custom-call | flops 21474836480 | bytes 1048576 | tf_op jit(solution)/shard_map/pack/pallas_call | solution.py:296
  1.4 0.0 copy-start.5
  1.4 0.0 copy-start.6
  1.5 13.9 %all_to_all.10.request_ref = f32[16,4,128]{2,1,0:T(4,128)S(1)} all-to-all(f32[16,4,128]{2,1,0:T(4,128)S(1)} %get-tuple-element.9), channel_id=1, replica_groups=mesh['runs'=2,'brick'=16] {'brick'}, dimensions={0} | all-to-all | bytes 65536 | tf_op jit(solution)/shard_map/all_to_all | solution.py:314
  15.3 0.0 copy-done
  15.3 0.0 copy-done.1
  15.3 0.0 copy-done.2
  15.3 0.0 copy-done.3
  15.3 0.0 copy-done.4
  15.3 3.1 %sample.1 = (f32[16,2,128]{2,1,0:T(2,128)S(1)}, f32[192,512]{1,0:T(8,128)S(1)}) custom-call(f32[16,4,128]{2,1,0:T(4,128)S(1)} %all_to_all.10.request_ref, f32[2048,3,128]{2,1,0:T(4,128)S(1)} %bitcast.5, f32[64,512]{1,0:T(8,128)S(1)} %copy-done.1, f32[64,64]{1,0:T(8,128)S(1)} %copy-done.2, f32[64,64]{1,0:T(8,128)S(1)} %copy-done.3, f32[64,64]{1,0:T(8,128)S(1)} %copy-done.4), custom_call_target="tpu_custom_call" | custom-call | tf_op jit(solution)/shard_map/sample/pallas_call | solution.py:317
  18.4 9.1 %all_to_all.11.reply_ref = f32[16,2,128]{2,1,0:T(2,128)S(1)} all-to-all(f32[16,2,128]{2,1,0:T(2,128)S(1)} %get-tuple-element.10), channel_id=1, replica_groups=mesh['runs'=2,'brick'=16] {'brick'}, dimensions={0} | all-to-all | bytes 32768 | tf_op jit(solution)/shard_map/all_to_all | solution.py:336
  27.5 0.0 copy-done.5
  27.5 0.0 copy-done.6
  27.5 1.9 %advance.1 = f32[64,512]{1,0:T(8,128)} custom-call(f32[16,2,128]{2,1,0:T(2,128)S(1)} %all_to_all.11.reply_ref, f32[192,512]{1,0:T(8,128)S(1)} %get-tuple-element.11.first_ref, s32[1,512]{1,0:T(1,128)S(1)} %bitcast.7, s32[1,512]{1,0:T(1,128)S(1)} %get-tuple-element.12.rank_ref, s32[1,512]{1,0:T(1,128)S(1)} %bitcast.8, f32[64,512]{1,0:T(8,128)S(1)} %copy-done.1, ...), custom_call_target="tpu_custom_call" | custom-call | tf_op jit(solution)/shard_map/advance/pallas_call | solution.py:337
Async XLA Ops:
  0.0 15.3 %copy-start = (f32[3,262144]{1,0:T(4,128)S(1)}, f32[3,262144]{1,0:T(4,128)}, u32[]{:S(2)}) copy-start(f32[3,262144]{1,0:T(4,128)} %param.9) | copy-start | bytes 9437188
  0.0 15.3 %copy-start.1 = (f32[64,512]{1,0:T(8,128)S(1)}, f32[64,512]{1,0:T(8,128)}, u32[]{:S(2)}) copy-start(f32[64,512]{1,0:T(8,128)} %dist_ref.3) | copy-start | bytes 393220
  0.0 15.3 %copy-start.2 = (f32[64,64]{1,0:T(8,128)S(1)}, f32[64,64]{1,0:T(8,128)}, u32[]{:S(2)}) copy-start(f32[64,64]{1,0:T(8,128)} %kernel_ref.3) | copy-start | bytes 49156
  0.0 15.3 %copy-start.3 = (f32[64,64]{1,0:T(8,128)S(1)}, f32[64,64]{1,0:T(8,128)}, u32[]{:S(2)}) copy-start(f32[64,64]{1,0:T(8,128)} %redist_ref.3) | copy-start | bytes 49156
  0.0 15.3 %copy-start.4 = (f32[64,64]{1,0:T(8,128)S(1)}, f32[64,64]{1,0:T(8,128)}, u32[]{:S(2)}) copy-start(f32[64,64]{1,0:T(8,128)} %shatter_ref.3) | copy-start | bytes 49156
  1.4 26.1 %copy-start.5 = (s32[512,1]{0,1:T(1,128)S(1)}, s32[512,1]{0,1:T(1,128)}, u32[]{:S(2)}) copy-start(s32[512,1]{0,1:T(1,128)} %param.11) | copy-start | bytes 6148
  1.4 26.1 %copy-start.6 = (s32[512]{0:T(512)S(1)}, s32[512]{0:T(512)}, u32[]{:S(2)}) copy-start(s32[512]{0:T(512)} %param.14) | copy-start | bytes 6148

commit v3 on v2

--- a/solution.py
+++ b/solution.py
@@ -78,11 +78,8 @@
     row = lax.broadcasted_iota(jnp.int32, (LANES, 2 * LANES), 0)
     column = lax.broadcasted_iota(jnp.int32, (LANES, 2 * LANES), 1)
     before = jnp.where((row < column) | (column >= LANES), 1.0, 0.0).astype(jnp.bfloat16)
-    lane = lax.broadcasted_iota(jnp.int32, (LANES, tracers), 0)
-    place = (lane % capacity).astype(jnp.float32)
-    left = lane < HALF
-    nobody = jnp.full((LANES, tracers), -1.0, jnp.float32)
-    places = (jnp.where(left, place, nobody), jnp.where(left, nobody, place))
+    place = lax.broadcasted_iota(jnp.int32, (LANES, tracers), 0) % capacity
+    place = place.astype(jnp.float32)
     copies[0].wait()
     owner = owner_ref[...]
     member = [
@@ -101,26 +98,29 @@
         base = base + block[:, LANES:]
     rank = jnp.concatenate(ranks, axis=1)
     rank_ref[...] = rank.astype(jnp.int32)
-    places = [jnp.where(rank == x, 1.0, 0.0).astype(jnp.bfloat16) for x in places]
+    onehot = jnp.where(rank == place, 1.0, 0.0).astype(jnp.bfloat16)
     copies[1].wait()
     copies[2].wait()
     coords = coords_ref[...].astype(jnp.float32)
     hi, mid, low = split3(fracs_ref[...])
-    none = jnp.zeros((3, tracers), jnp.float32)
+    none = jnp.zeros((1, tracers), jnp.float32)
     rows = bricks * 4
     mine = owner == lax.broadcasted_iota(jnp.int32, (rows, tracers), 0) // 4
-    total = None
-    for x in (hi, mid, low):
-        first = coords if total is None else none
-        for onehot, lines in ((0, (first, x[:1])), (1, (x[1:], none[:2]))):
-            block = jnp.concatenate(lines, axis=0)
-            pair = jnp.concatenate([block, block], axis=0)
-            masked = jnp.concatenate([pair] * (bricks // 2), axis=0)
-            masked = jnp.where(mine, masked, 0.0).astype(jnp.bfloat16)
-            term = lax.dot_general(
-                masked, places[onehot], NT, preferred_element_type=jnp.float32
-            )
-            total = term if total is None else total + term
+
+    def placed(*lines):
+        block = jnp.concatenate(lines, axis=0)
+        pair = jnp.concatenate([block, block], axis=0)
+        masked = jnp.where(mine, jnp.concatenate([pair] * (bricks // 2), axis=0), 0.0)
+        return lax.dot_general(
+            masked.astype(jnp.bfloat16), onehot, NT, preferred_element_type=jnp.float32
+        )
+
+    cells = placed(coords, none)
+    fractions = [placed(x[1:], none, x[:1]) for x in (hi, mid, low)]
+    fractions = fractions[0] + fractions[1] + fractions[2]
+    row = lax.broadcasted_iota(jnp.int32, (rows, LANES), 0) % 4
+    lane = lax.broadcasted_iota(jnp.int32, (rows, LANES), 1)
+    total = jnp.where((row < 3) & (lane < HALF), cells, fractions)
     for b in range(bricks):
         request_ref[b] = total[4 * b : 4 * b + 4]
 

time: 29.6 us -> 29.6 us (level)
  no operation moved by 1% of the time
where the time goes in v3:
time: 29.6 us; the launch traced here: 29.4 us
  blocking collectives  23.1 us (78%)
  Pallas kernels  6.27 us (21%)
    all_to_all x1, blocking collectives, shards(): lax.all_to_all(request, 'brick', split_axis=0, concat_axis=0, tiled=True)  14 us
    all_to_all x1, blocking collectives, shards(): lax.all_to_all(reply, 'brick', split_axis=0, concat_axis=0, tiled=True)  9.07 us
    pallas_call x1, Pallas kernels, shards(): pl.pallas_call(functools.partial(sample_kernel, bricks, capacity), out_sh...  3.09 us
    pallas_call x1, Pallas kernels, shards(): pl.pallas_call(functools.partial(advance_kernel, bricks, capacity), out_s...  1.85 us
    pallas_call x1, Pallas kernels, shards(): pl.pallas_call(functools.partial(pack_kernel, bricks, capacity), out_shap...  1.32 us

profile of v3, /device:TPU:0, one launch (start us, length us, event | category | flops | bytes accessed | tf_op | source)
XLA Modules:
  0.0 29.4 jit_solution(3965177187677692308)
XLA Ops:
  0.0 0.0 copy-start
  0.0 0.0 copy-start.1
  0.0 0.0 copy-start.2
  0.0 0.0 copy-start.3
  0.0 0.0 copy-start.4
  0.0 1.3 %pack.1 = (f32[16,4,128]{2,1,0:T(4,128)S(1)}, s32[1,512]{1,0:T(1,128)S(1)}) custom-call(s32[1,512]{1,0:T(1,128)} %bitcast.6, s32[3,512]{1,0:T(4,128)} %coords_hbm.1, f32[3,512]{1,0:T(4,128)} %fracs_hbm.1), custom_call_target="tpu_custom_call" | custom-call | flops 21474836480 | bytes 1048576 | tf_op jit(solution)/shard_map/pack/pallas_call | solution.py:296
  1.3 0.0 copy-start.5
  1.4 0.0 copy-start.6
  1.4 14.0 %all_to_all.10.request_ref = f32[16,4,128]{2,1,0:T(4,128)S(1)} all-to-all(f32[16,4,128]{2,1,0:T(4,128)S(1)} %get-tuple-element.9), channel_id=1, replica_groups=mesh['runs'=2,'brick'=16] {'brick'}, dimensions={0} | all-to-all | bytes 65536 | tf_op jit(solution)/shard_map/all_to_all | solution.py:314
  15.4 0.0 copy-done
  15.4 0.0 copy-done.1
  15.4 0.0 copy-done.2
  15.4 0.0 copy-done.3
  15.4 0.0 copy-done.4
  15.4 3.1 %sample.1 = (f32[16,2,128]{2,1,0:T(2,128)S(1)}, f32[192,512]{1,0:T(8,128)S(1)}) custom-call(f32[16,4,128]{2,1,0:T(4,128)S(1)} %all_to_all.10.request_ref, f32[2048,3,128]{2,1,0:T(4,128)S(1)} %bitcast.5, f32[64,512]{1,0:T(8,128)S(1)} %copy-done.1, f32[64,64]{1,0:T(8,128)S(1)} %copy-done.2, f32[64,64]{1,0:T(8,128)S(1)} %copy-done.3, f32[64,64]{1,0:T(8,128)S(1)} %copy-done.4), custom_call_target="tpu_custom_call" | custom-call | tf_op jit(solution)/shard_map/sample/pallas_call | solution.py:317
  18.5 9.1 %all_to_all.11.reply_ref = f32[16,2,128]{2,1,0:T(2,128)S(1)} all-to-all(f32[16,2,128]{2,1,0:T(2,128)S(1)} %get-tuple-element.10), channel_id=1, replica_groups=mesh['runs'=2,'brick'=16] {'brick'}, dimensions={0} | all-to-all | bytes 32768 | tf_op jit(solution)/shard_map/all_to_all | solution.py:336
  27.6 0.0 copy-done.5
  27.6 0.0 copy-done.6
  27.6 1.9 %advance.1 = f32[64,512]{1,0:T(8,128)} custom-call(f32[16,2,128]{2,1,0:T(2,128)S(1)} %all_to_all.11.reply_ref, f32[192,512]{1,0:T(8,128)S(1)} %get-tuple-element.11.first_ref, s32[1,512]{1,0:T(1,128)S(1)} %bitcast.7, s32[1,512]{1,0:T(1,128)S(1)} %get-tuple-element.12.rank_ref, s32[1,512]{1,0:T(1,128)S(1)} %bitcast.8, f32[64,512]{1,0:T(8,128)S(1)} %copy-done.1, ...), custom_call_target="tpu_custom_call" | custom-call | tf_op jit(solution)/shard_map/advance/pallas_call | solution.py:337
Async XLA Ops:
  0.0 15.4 %copy-start = (f32[3,262144]{1,0:T(4,128)S(1)}, f32[3,262144]{1,0:T(4,128)}, u32[]{:S(2)}) copy-start(f32[3,262144]{1,0:T(4,128)} %param.9) | copy-start | bytes 9437188
  0.0 15.4 %copy-start.1 = (f32[64,512]{1,0:T(8,128)S(1)}, f32[64,512]{1,0:T(8,128)}, u32[]{:S(2)}) copy-start(f32[64,512]{1,0:T(8,128)} %dist_ref.3) | copy-start | bytes 393220
  0.0 15.4 %copy-start.2 = (f32[64,64]{1,0:T(8,128)S(1)}, f32[64,64]{1,0:T(8,128)}, u32[]{:S(2)}) copy-start(f32[64,64]{1,0:T(8,128)} %kernel_ref.3) | copy-start | bytes 49156
  0.0 15.4 %copy-start.3 = (f32[64,64]{1,0:T(8,128)S(1)}, f32[64,64]{1,0:T(8,128)}, u32[]{:S(2)}) copy-start(f32[64,64]{1,0:T(8,128)} %redist_ref.3) | copy-start | bytes 49156
  0.0 15.4 %copy-start.4 = (f32[64,64]{1,0:T(8,128)S(1)}, f32[64,64]{1,0:T(8,128)}, u32[]{:S(2)}) copy-start(f32[64,64]{1,0:T(8,128)} %shatter_ref.3) | copy-start | bytes 49156
  1.3 26.2 %copy-start.5 = (s32[512,1]{0,1:T(1,128)S(1)}, s32[512,1]{0,1:T(1,128)}, u32[]{:S(2)}) copy-start(s32[512,1]{0,1:T(1,128)} %param.11) | copy-start | bytes 6148
  1.4 26.2 %copy-start.6 = (s32[512]{0:T(512)S(1)}, s32[512]{0:T(512)}, u32[]{:S(2)}) copy-start(s32[512]{0:T(512)} %param.14) | copy-start | bytes 6148

commit v4 on v2

--- a/solution.py
+++ b/solution.py
@@ -136,6 +136,8 @@
     shatter_ref,
     reply_ref,
     first_ref,
+    both_out,
+    redist_out,
     staged,
     code_ref,
     frac_ref,
@@ -206,6 +208,8 @@
     former = lax.broadcasted_iota(jnp.int32, (4, LANES), 1) < HALF
     bins = dist_ref.shape[0]
     both, redist = tables(kernel_ref, redist_ref, shatter_ref)
+    both_out[...] = both
+    redist_out[...] = redist
     for k, value in enumerate(collide(both, redist, dist_ref[...])):
         first_ref[k * bins : (k + 1) * bins] = value
     for copy in early:
@@ -245,9 +249,8 @@
     rank_ref,
     counts_ref,
     dist_ref,
-    kernel_ref,
+    both_ref,
     redist_ref,
-    shatter_ref,
     out_ref,
 ):
     tracers = owner_ref.shape[1]
@@ -272,7 +275,7 @@
     h = 1.0 / jnp.maximum(counts, 1).astype(jnp.float32)
 
     bins = dist_ref.shape[0]
-    both, redist = tables(kernel_ref, redist_ref, shatter_ref)
+    both, redist = both_ref[...], redist_ref[...]
     hcoag = h * coag
     hshat = h * shat
     n = dist_ref[...]
@@ -314,14 +317,17 @@
     asked = lax.all_to_all(request, "brick", split_axis=0, concat_axis=0, tiled=True)
     cells = grid.shape[1]
     tiles = grid.reshape(3, cells // LANES, LANES).transpose(1, 0, 2)
-    reply, first = pl.pallas_call(
+    bins = distribution.shape[0]
+    reply, first, both, moving = pl.pallas_call(
         functools.partial(sample_kernel, bricks, capacity),
         out_shape=(
             jax.ShapeDtypeStruct((bricks, blocks, LANES), jnp.float32),
-            jax.ShapeDtypeStruct((3 * distribution.shape[0], tracers), jnp.float32),
+            jax.ShapeDtypeStruct((3 * bins, tracers), jnp.float32),
+            jax.ShapeDtypeStruct((2 * bins, 3 * bins), jnp.bfloat16),
+            jax.ShapeDtypeStruct((bins, 3 * bins), jnp.bfloat16),
         ),
         in_specs=[vmem] * 6,
-        out_specs=(vmem, vmem),
+        out_specs=(vmem,) * 4,
         scratch_shapes=[
             pltpu.VMEM((bricks, 4, LANES), jnp.int32),
             pltpu.SMEM((bricks, LANES), jnp.int32),
@@ -337,11 +343,11 @@
     return pl.pallas_call(
         functools.partial(advance_kernel, bricks, capacity),
         out_shape=jax.ShapeDtypeStruct(distribution.shape, jnp.float32),
-        in_specs=[vmem] * 9,
+        in_specs=[vmem] * 8,
         out_specs=vmem,
         compiler_params=pltpu.CompilerParams(vmem_limit_bytes=8 << 20),
         name="advance",
-    )(back, first, owner, rank, counts.reshape(1, tracers), distribution, kernel, redist, shatter)
+    )(back, first, owner, rank, counts.reshape(1, tracers), distribution, both, moving)
 
 
 def solution(mesh):

time: 29.6 us -> 29.6 us (level)
  no operation moved by 1% of the time
where the time goes in v4:
time: 29.6 us; the launch traced here: 29.4 us
  blocking collectives  22.9 us (77%)
  Pallas kernels  6.36 us (21%)
    all_to_all x1, blocking collectives, shards(): lax.all_to_all(request, 'brick', split_axis=0, concat_axis=0, tiled=True)  13.9 us
    all_to_all x1, blocking collectives, shards(): lax.all_to_all(reply, 'brick', split_axis=0, concat_axis=0, tiled=True)  9.07 us
    pallas_call x1, Pallas kernels, shards(): pl.pallas_call(functools.partial(sample_kernel, bricks, capacity), out_sh...  3.09 us
    pallas_call x1, Pallas kernels, shards(): pl.pallas_call(functools.partial(advance_kernel, bricks, capacity), out_s...  1.86 us
    pallas_call x1, Pallas kernels, shards(): pl.pallas_call(functools.partial(pack_kernel, bricks, capacity), out_shap...  1.41 us

profile of v4, /device:TPU:0, one launch (start us, length us, event | category | flops | bytes accessed | tf_op | source)
XLA Modules:
  0.0 29.4 jit_solution(8506977127132659853)
XLA Ops:
  0.0 0.0 copy-start
  0.0 0.0 copy-start.1
  0.0 0.0 copy-start.2
  0.0 0.0 copy-start.3
  0.0 0.0 copy-start.4
  0.0 1.4 %pack.1 = (f32[16,4,128]{2,1,0:T(4,128)S(1)}, s32[1,512]{1,0:T(1,128)S(1)}) custom-call(s32[1,512]{1,0:T(1,128)} %bitcast.6, s32[3,512]{1,0:T(4,128)} %coords_hbm.1, f32[3,512]{1,0:T(4,128)} %fracs_hbm.1), custom_call_target="tpu_custom_call" | custom-call | flops 21474836480 | bytes 1048576 | tf_op jit(solution)/shard_map/pack/pallas_call | solution.py:299
  1.4 0.0 copy-start.5
  1.4 0.0 copy-start.6
  1.5 13.9 %all_to_all.10.request_ref = f32[16,4,128]{2,1,0:T(4,128)S(1)} all-to-all(f32[16,4,128]{2,1,0:T(4,128)S(1)} %get-tuple-element.11), channel_id=1, replica_groups=mesh['runs'=2,'brick'=16] {'brick'}, dimensions={0} | all-to-all | bytes 65536 | tf_op jit(solution)/shard_map/all_to_all | solution.py:317
  15.3 0.0 copy-done
  15.3 0.0 copy-done.1
  15.3 0.0 copy-done.2
  15.3 0.0 copy-done.3
  15.3 0.0 copy-done.4
  15.3 3.1 %sample.1 = (f32[16,2,128]{2,1,0:T(2,128)S(1)}, f32[192,512]{1,0:T(8,128)S(1)}, bf16[128,192]{1,0:T(8,128)(2,1)S(1)}, bf16[64,192]{1,0:T(8,128)(2,1)S(1)}) custom-call(f32[16,4,128]{2,1,0:T(4,128)S(1)} %all_to_all.10.request_ref, f32[2048,3,128]{2,1,0:T(4,128)S(1)} %bitcast.5, f32[64,512]{1,0:T(8,128)S(1)} %copy-done.1, f32[64,64]{1,0:T(8,128)S(1)} %copy-done.2, ...), custom_call_target="tpu_custom_call" | custom-call | tf_op jit(solution)/shard_map/sample/pallas_call | solution.py:321
  18.4 9.1 %all_to_all.11.reply_ref = f32[16,2,128]{2,1,0:T(2,128)S(1)} all-to-all(f32[16,2,128]{2,1,0:T(2,128)S(1)} %get-tuple-element.12), channel_id=1, replica_groups=mesh['runs'=2,'brick'=16] {'brick'}, dimensions={0} | all-to-all | bytes 32768 | tf_op jit(solution)/shard_map/all_to_all | solution.py:342
  27.5 0.0 copy-done.5
  27.5 0.0 copy-done.6
  27.5 1.9 %advance.1 = f32[64,512]{1,0:T(8,128)} custom-call(f32[16,2,128]{2,1,0:T(2,128)S(1)} %all_to_all.11.reply_ref, f32[192,512]{1,0:T(8,128)S(1)} %get-tuple-element.13.first_ref, s32[1,512]{1,0:T(1,128)S(1)} %bitcast.7, s32[1,512]{1,0:T(1,128)S(1)} %get-tuple-element.14.rank_ref, s32[1,512]{1,0:T(1,128)S(1)} %bitcast.8, f32[64,512]{1,0:T(8,128)S(1)} %copy-done.1, ...), custom_call_target="tpu_custom_call" | custom-call | tf_op jit(solution)/shard_map/advance/pallas_call | solution.py:343
Async XLA Ops:
  0.0 15.3 %copy-start = (f32[3,262144]{1,0:T(4,128)S(1)}, f32[3,262144]{1,0:T(4,128)}, u32[]{:S(2)}) copy-start(f32[3,262144]{1,0:T(4,128)} %param.9) | copy-start | bytes 9437188
  0.0 15.3 %copy-start.1 = (f32[64,512]{1,0:T(8,128)S(1)}, f32[64,512]{1,0:T(8,128)}, u32[]{:S(2)}) copy-start(f32[64,512]{1,0:T(8,128)} %dist_ref.3) | copy-start | bytes 393220
  0.0 15.3 %copy-start.2 = (f32[64,64]{1,0:T(8,128)S(1)}, f32[64,64]{1,0:T(8,128)}, u32[]{:S(2)}) copy-start(f32[64,64]{1,0:T(8,128)} %kernel_ref.1) | copy-start | bytes 49156
  0.0 15.3 %copy-start.3 = (f32[64,64]{1,0:T(8,128)S(1)}, f32[64,64]{1,0:T(8,128)}, u32[]{:S(2)}) copy-start(f32[64,64]{1,0:T(8,128)} %redist_ref.1) | copy-start | bytes 49156
  0.0 15.3 %copy-start.4 = (f32[64,64]{1,0:T(8,128)S(1)}, f32[64,64]{1,0:T(8,128)}, u32[]{:S(2)}) copy-start(f32[64,64]{1,0:T(8,128)} %shatter_ref.1) | copy-start | bytes 49156
  1.4 26.1 %copy-start.5 = (s32[512,1]{0,1:T(1,128)S(1)}, s32[512,1]{0,1:T(1,128)}, u32[]{:S(2)}) copy-start(s32[512,1]{0,1:T(1,128)} %param.11) | copy-start | bytes 6148
  1.4 26.1 %copy-start.6 = (s32[512]{0:T(512)S(1)}, s32[512]{0:T(512)}, u32[]{:S(2)}) copy-start(s32[512]{0:T(512)} %param.14) | copy-start | bytes 6148
